TPU v7x, 8 devices: a whole 2x2x1 slice. The times are simulated.
8 devices in a mesh: dp: 1 (over z), sub: 2 (over y), ep: 4 (over x, core).
Axes of the slice: x: 2, y: 2, z: 1, core: 2. Of those that a mesh axis runs over, the one named last changes fastest.
Arguments:
- input_a: bfloat16 [8, 512, 4096], P(('dp', 'ep', 'sub'))
- input_b: bfloat16 [8, 512, 4096], P(('dp', 'ep', 'sub'))
- route_idx: int32 [2, 4096, 8], P(None, ('dp', 'ep', 'sub'))
- route_gate: float32 [2, 4096, 8], P(None, ('dp', 'ep', 'sub'))
- attn_norm: float32 [4096], replicated
- w_query: bfloat16 [4096, 64, 128], replicated
- w_key: bfloat16 [4096, 64, 128], replicated
- w_value: bfloat16 [4096, 64, 128], replicated
- w_out: bfloat16 [64, 128, 4096], replicated
- moe_norm: float32 [4096], replicated
- w_gate: bfloat16 [16, 4096, 1536], P(('ep', 'sub'))
- w_up: bfloat16 [16, 4096, 1536], P(('ep', 'sub'))
- w_down: bfloat16 [16, 1536, 4096], P(('ep', 'sub'))
Outputs:
- output 1: bfloat16 [8, 512, 4096], P(('dp', 'ep', 'sub'))
- output 2: bfloat16 [8, 512, 4096], P(('dp', 'ep', 'sub'))
All inputs are finite; a program needn't handle non-finite values.
Results may differ from a plain program's by a relative error of at most 0.0126636.
Values are sent between devices in bfloat16 or wider.
A program may use at most 1.5 GiB of HBM per device.

v0:
```python
import jax
import jax.numpy as jnp
from jax import lax
from jax.sharding import PartitionSpec as P

NORM_EPS = 1e-6


def rms_norm(values, norm_gain):
    acc_f32 = values.astype(jnp.float32)
    inv_rms = lax.rsqrt(jnp.mean(acc_f32 * acc_f32, axis=-1, keepdims=True) + NORM_EPS)
    return (acc_f32 * inv_rms * norm_gain).astype(jnp.bfloat16)


def attention_block(tokens, attn_norm, w_query, w_key, w_value, w_out):
    normed = rms_norm(tokens, attn_norm)
    q_heads = jnp.einsum('bsd,dhc->bshc', normed, w_query, preferred_element_type=jnp.float32).astype(jnp.bfloat16)
    k_heads = jnp.einsum('bsd,dhc->bshc', normed, w_key, preferred_element_type=jnp.float32).astype(jnp.bfloat16)
    v_heads = jnp.einsum('bsd,dhc->bshc', normed, w_value, preferred_element_type=jnp.float32).astype(jnp.bfloat16)
    score_scale = w_query.shape[2] ** -0.5
    scores = jnp.einsum('bqhc,bkhc->bhqk', q_heads, k_heads, preferred_element_type=jnp.float32) * score_scale
    seq_len = tokens.shape[1]
    causal = lax.broadcasted_iota(jnp.int32, (seq_len, seq_len), 0) >= lax.broadcasted_iota(jnp.int32, (seq_len, seq_len), 1)
    scores = jnp.where(causal, scores, -jnp.inf)
    prob_bf = jax.nn.softmax(scores, axis=-1).astype(jnp.bfloat16)
    context = jnp.einsum('bhqk,bkhc->bqhc', prob_bf, v_heads, preferred_element_type=jnp.float32).astype(jnp.bfloat16)
    proj_out = jnp.einsum('crid,ide->cre', context, w_out, preferred_element_type=jnp.float32)
    return (tokens.astype(jnp.float32) + proj_out).astype(jnp.bfloat16)


def route_slots(exp_ids, num_exp, cap_slots):
    tok_count, top_k = exp_ids.shape
    flat_ids = exp_ids.reshape(-1)
    sort_order = jnp.argsort(flat_ids, stable=True)
    sorted_ids = flat_ids[sort_order]
    counts = jnp.bincount(flat_ids, length=num_exp)
    starts = jnp.cumsum(counts) - counts
    slot_rank = jnp.arange(flat_ids.shape[0], dtype=jnp.int32) - starts[sorted_ids]
    slot_sorted = sorted_ids * cap_slots + slot_rank
    slot_of = jnp.zeros_like(flat_ids).at[sort_order].set(slot_sorted)
    holder = jnp.full((num_exp * cap_slots,), tok_count, jnp.int32).at[slot_sorted].set(sort_order // top_k)
    return slot_of, holder


def expert_ffn(disp_rows, w_gate, w_up, w_down):
    gate_h = jnp.einsum('end,edf->enf', disp_rows, w_gate, preferred_element_type=jnp.float32)
    up_h = jnp.einsum('end,edf->enf', disp_rows, w_up, preferred_element_type=jnp.float32)
    act_rows = (jax.nn.silu(gate_h) * up_h).astype(jnp.bfloat16)
    return jnp.einsum('enf,efd->end', act_rows, w_down, preferred_element_type=jnp.float32).astype(jnp.bfloat16)


def micro_step(tokens, exp_ids, gate_w, attn_norm, w_query, w_key, w_value, w_out, moe_norm, w_gate, w_up, w_down, ep_size, sub_size):
    hidden = attention_block(tokens, attn_norm, w_query, w_key, w_value, w_out)
    seq_count, seq_len, model_dim = hidden.shape
    flat_tok = hidden.reshape(seq_count * seq_len, model_dim)
    tok_count, top_k = exp_ids.shape
    exp_local = w_gate.shape[0]
    num_exp = exp_local * ep_size * sub_size
    cap_slots = 3 * top_k * tok_count // (2 * num_exp)
    normed = rms_norm(flat_tok, moe_norm)
    slot_of, holder = route_slots(exp_ids, num_exp, cap_slots)
    send_buf = jnp.take(normed, holder, axis=0, mode='fill', fill_value=0)
    send_buf = send_buf.reshape(ep_size, sub_size, exp_local, cap_slots, model_dim)
    across_ep = lax.all_to_all(send_buf, 'ep', 0, 3, tiled=True)
    arrived = lax.all_to_all(across_ep, 'sub', 1, 3, tiled=True)
    expert_out = expert_ffn(arrived.reshape(exp_local, -1, model_dim), w_gate, w_up, w_down)
    back_sub = lax.all_to_all(expert_out.reshape(1, 1, exp_local, -1, model_dim), 'sub', 3, 1, tiled=True)
    returned = lax.all_to_all(back_sub, 'ep', 3, 0, tiled=True)
    picked = jnp.take(returned.reshape(num_exp * cap_slots, model_dim), slot_of, axis=0).reshape(tok_count, top_k, model_dim)
    moe_sum = jnp.sum(gate_w[:, :, None] * picked.astype(jnp.float32), axis=1)
    out_tok = (flat_tok.astype(jnp.float32) + moe_sum).astype(jnp.bfloat16)
    return out_tok.reshape(seq_count, seq_len, model_dim)


def solution(mesh):
    ep_size = mesh.shape['ep']
    sub_size = mesh.shape['sub']
    tok_spec = P(('dp', 'ep', 'sub'), None, None)
    route_spec = P(None, ('dp', 'ep', 'sub'), None)
    exp_spec = P(('ep', 'sub'), None, None)

    def device_body(input_a, input_b, route_idx, route_gate, attn_norm, w_query, w_key, w_value, w_out, moe_norm, w_gate, w_up, w_down):
        out_a = micro_step(input_a, route_idx[0], route_gate[0], attn_norm, w_query, w_key, w_value, w_out, moe_norm, w_gate, w_up, w_down, ep_size, sub_size)
        out_b = micro_step(input_b, route_idx[1], route_gate[1], attn_norm, w_query, w_key, w_value, w_out, moe_norm, w_gate, w_up, w_down, ep_size, sub_size)
        return out_a, out_b

    return jax.shard_map(device_body, mesh=mesh, in_specs=(tok_spec, tok_spec, route_spec, route_spec, P(), P(), P(), P(), P(), P(), exp_spec, exp_spec, exp_spec), out_specs=(tok_spec, tok_spec), check_vma=False)
```

profile of v0, /device:TPU:0, one launch (start us, length us, event | category | flops | bytes accessed | tf_op | source)
XLA Modules:
  0.0 5874.0 jit_solution(5118180062898441858)
XLA Ops:
  4.5 42.2 fusion.10
  46.7 41.2 fusion.168
  88.8 41.5 fusion.8
  171.4 41.1 fusion.14
  370.8 65.9 %fusion.118 = (f32[64,512]{1,0:T(8,128)S(1)}, f32[64,512,512]{1,2,0:T(8,128)}) fusion(f32[64,512,512]{1,2,0:T(8,128)} %fusion.63, pred[512,512]{0,1:T(8,128)(4,1)S(1)} %copy-done.3), kind=kOutput, calls=%fused_computation.199 | output fusion | flops 100663808 | bytes 134610944 | tf_op jit(solution)/shard_map/sub | solution.py:25
  465.5 66.0 %fusion.119 = (f32[64,512]{1,0:T(8,128)S(1)}, f32[64,512,512]{1,2,0:T(8,128)}) fusion(f32[64,512,512]{1,2,0:T(8,128)} %fusion.53, pred[512,512]{0,1:T(8,128)(4,1)S(1)} %copy-done.3), kind=kOutput, calls=%fused_computation.200 | output fusion | flops 100663808 | bytes 134610944 | tf_op jit(solution)/shard_map/sub | solution.py:25
  559.9 45.2 fusion.32
  633.0 45.5 fusion.36
  685.7 85.7 %gather_fusion.2 = bf16[6144,4096]{1,0:T(8,128)(2,1)} fusion(bf16[512,4096]{1,0:T(8,128)(2,1)} %get-tuple-element.44, s32[6144]{0:T(1024)S(1)} %copy-done.4), kind=kCustom, calls=%fused_computation.clone | custom fusion | bytes 100687872 | tf_op jit(solution)/shard_map/jit(_take)/gather | solution.py:62
  903.7 85.7 %gather_fusion.4 = bf16[6144,4096]{1,0:T(8,128)(2,1)} fusion(bf16[512,4096]{1,0:T(8,128)(2,1)} %get-tuple-element.43, s32[6144]{0:T(1024)S(1)} %fusion.83), kind=kCustom, calls=%fused_computation.2.clone | custom fusion | bytes 100687872 | tf_op jit(solution)/shard_map/jit(_take)/gather | solution.py:62
  1022.8 337.5 %all-to-all-done = bf16[4,2,2,384,4096]{4,3,2,1,0:T(8,128)(2,1)} async-done(((bf16[4,2,2,384,4096]{4,3,2,1,0:T(8,128)(2,1)}), bf16[4,2,2,384,4096]{4,3,2,1,0:T(8,128)(2,1)}, u32[]{:S(2)}, u32[]{:S(2)}) %all-to-all-start) | async-done | bytes 50331680 | tf_op jit(solution)/shard_map/all_to_all | solution.py:64
  1405.1 509.2 %all-to-all-done.4 = bf16[4,2,2,384,4096]{4,3,2,1,0:T(8,128)(2,1)} async-done(((bf16[4,2,2,384,4096]{4,3,2,1,0:T(8,128)(2,1)}), bf16[4,2,2,384,4096]{4,3,2,1,0:T(8,128)(2,1)}, u32[]{:S(2)}, u32[]{:S(2)}) %all-to-all-start.4) | async-done | bytes 50331680 | tf_op jit(solution)/shard_map/all_to_all | solution.py:64
  1966.0 509.0 %all-to-all-done.1 = bf16[1,2,2,1536,4096]{4,3,2,0,1:T(8,128)(2,1)} async-done(((bf16[1,2,2,1536,4096]{4,3,2,0,1:T(8,128)(2,1)}), bf16[1,2,2,1536,4096]{4,3,2,0,1:T(8,128)(2,1)}, u32[]{:S(2)}, u32[]{:S(2)}) %all-to-all-start.1) | async-done | bytes 50331680 | tf_op jit(solution)/shard_map/all_to_all | solution.py:65
  2526.9 88.3 %fusion.121 = f32[2,3072,1536]{2,1,0:T(8,128)} fusion(bf16[2,3072,4096]{2,1,0:T(8,128)(2,1)} %bitcast.212, bf16[2,4096,1536]{2,1,0:T(8,128)(2,1)} %param.28), kind=kOutput, calls=%fused_computation.202 | convolution fusion | flops 77309411328 | bytes 113246208 | tf_op jit(solution)/shard_map/end,edf->enf/dot_general | solution.py:47
  2615.2 88.8 %fusion.120 = f32[2,3072,1536]{2,1,0:T(8,128)} fusion(bf16[2,3072,4096]{2,1,0:T(8,128)(2,1)} %bitcast.213, bf16[2,4096,1536]{2,1,0:T(8,128)(2,1)} %param.27), kind=kOutput, calls=%fused_computation.201 | convolution fusion | flops 77309411328 | bytes 113246208 | tf_op jit(solution)/shard_map/end,edf->enf/dot_general | solution.py:46
  2703.9 330.7 %all-to-all-done.5 = bf16[1,2,2,1536,4096]{4,3,2,0,1:T(8,128)(2,1)} async-done(((bf16[1,2,2,1536,4096]{4,3,2,0,1:T(8,128)(2,1)}), bf16[1,2,2,1536,4096]{4,3,2,0,1:T(8,128)(2,1)}, u32[]{:S(2)}, u32[]{:S(2)}) %all-to-all-start.5) | async-done | bytes 50331680 | tf_op jit(solution)/shard_map/all_to_all | solution.py:65
  3068.4 88.5 %fusion.123 = f32[2,3072,1536]{2,1,0:T(8,128)} fusion(bf16[2,3072,4096]{2,1,0:T(8,128)(2,1)} %bitcast.214, bf16[2,4096,1536]{2,1,0:T(8,128)(2,1)} %param.28), kind=kOutput, calls=%fused_computation.204 | convolution fusion | flops 77309411328 | bytes 113246208 | tf_op jit(solution)/shard_map/end,edf->enf/dot_general | solution.py:47
  3156.8 88.5 %fusion.122 = f32[2,3072,1536]{2,1,0:T(8,128)} fusion(bf16[2,3072,4096]{2,1,0:T(8,128)(2,1)} %bitcast.215, bf16[2,4096,1536]{2,1,0:T(8,128)(2,1)} %param.27), kind=kOutput, calls=%fused_computation.203 | convolution fusion | flops 77309411328 | bytes 113246208 | tf_op jit(solution)/shard_map/end,edf->enf/dot_general | solution.py:46
  3245.3 94.2 %convert_bitcast_fusion.1 = bf16[1,1,2,3072,4096]{4,3,2,1,0:T(8,128)(2,1)} fusion(bf16[2,1536,4096]{2,1,0:T(8,128)(2,1)} %param.29, f32[2,3072,1536]{2,1,0:T(8,128)} %fusion.121, f32[2,3072,1536]{2,1,0:T(8,128)} %fusion.120), kind=kOutput, calls=%fused_computation.41 | convolution fusion | flops 77391200256 | bytes 150994944 | tf_op jit(solution)/shard_map/enf,efd->end/dot_general | solution.py:49
  3339.5 89.7 %copy.55 = bf16[1,1,2,3072,4096]{4,2,1,0,3:T(2,128)(2,1)} copy(bf16[1,1,2,3072,4096]{4,3,2,1,0:T(8,128)(2,1)} %convert_bitcast_fusion.1) | data formatting | bytes 100663296 | tf_op jit(solution)/shard_map/reshape | solution.py:67
  3447.9 94.3 %convert_bitcast_fusion = bf16[1,1,2,3072,4096]{4,3,2,1,0:T(8,128)(2,1)} fusion(bf16[2,1536,4096]{2,1,0:T(8,128)(2,1)} %param.29, f32[2,3072,1536]{2,1,0:T(8,128)} %fusion.123, f32[2,3072,1536]{2,1,0:T(8,128)} %fusion.122), kind=kOutput, calls=%fused_computation.40 | convolution fusion | flops 77391200256 | bytes 150994944 | tf_op jit(solution)/shard_map/enf,efd->end/dot_general | solution.py:49
  3542.2 89.2 %copy.70 = bf16[1,1,2,3072,4096]{4,2,1,0,3:T(2,128)(2,1)} copy(bf16[1,1,2,3072,4096]{4,3,2,1,0:T(8,128)(2,1)} %convert_bitcast_fusion) | data formatting | bytes 100663296 | tf_op jit(solution)/shard_map/reshape | solution.py:67
  3631.4 356.8 %all-to-all-done.2 = bf16[1,1,2,3072,4096]{4,2,1,0,3:T(2,128)(2,1)} async-done(((bf16[1,1,2,3072,4096]{4,2,1,0,3:T(2,128)(2,1)}), bf16[1,1,2,3072,4096]{4,2,1,0,3:T(2,128)(2,1)}, u32[]{:S(2)}, u32[]{:S(2)}) %all-to-all-start.2) | async-done | bytes 50331680 | tf_op jit(solution)/shard_map/all_to_all | solution.py:67
  4006.9 89.2 %copy.108 = bf16[1,1,2,2,1536,4096]{5,3,2,4,1,0:T(2,128)(2,1)} copy(bf16[1,1,2,2,1536,4096]{5,2,4,3,1,0:T(2,128)(2,1)} %bitcast.38) | data formatting | bytes 100663296 | tf_op jit(solution)/shard_map/all_to_all | solution.py:67
  4096.0 450.4 %all-to-all-done.6 = bf16[1,1,2,3072,4096]{4,2,1,0,3:T(2,128)(2,1)} async-done(((bf16[1,1,2,3072,4096]{4,2,1,0,3:T(2,128)(2,1)}), bf16[1,1,2,3072,4096]{4,2,1,0,3:T(2,128)(2,1)}, u32[]{:S(2)}, u32[]{:S(2)}) %all-to-all-start.6) | async-done | bytes 50331680 | tf_op jit(solution)/shard_map/all_to_all | solution.py:67
  4558.2 89.2 %copy.107 = bf16[1,1,2,2,1536,4096]{5,3,2,4,1,0:T(2,128)(2,1)} copy(bf16[1,1,2,2,1536,4096]{5,2,4,3,1,0:T(2,128)(2,1)} %bitcast.84) | data formatting | bytes 100663296 | tf_op jit(solution)/shard_map/all_to_all | solution.py:67
  4647.4 453.0 %all-to-all-done.3 = bf16[1,2,2,1536,4096]{4,1,2,0,3:T(2,128)(2,1)} async-done(((bf16[1,2,2,1536,4096]{4,1,2,0,3:T(2,128)(2,1)}), bf16[1,2,2,1536,4096]{4,1,2,0,3:T(2,128)(2,1)}, u32[]{:S(2)}, u32[]{:S(2)}) %all-to-all-start.3) | async-done | bytes 50331680 | tf_op jit(solution)/shard_map/all_to_all | solution.py:68
  5145.8 43.4 copy.57
  5189.2 133.2 %gather_fusion.3 = bf16[4096,4096]{1,0:T(8,128)(2,1)} fusion(bf16[6144,4096]{1,0:T(8,128)(2,1)} %bitcast.204, s32[4096]{0:T(1024)S(1)} %fusion.88), kind=kCustom, calls=%fused_computation.1.clone | custom fusion | bytes 67125248 | tf_op jit(solution)/shard_map/jit(_take)/gather | solution.py:69
  5364.4 290.1 %all-to-all-done.7 = bf16[1,2,2,1536,4096]{4,1,2,0,3:T(2,128)(2,1)} async-done(((bf16[1,2,2,1536,4096]{4,1,2,0,3:T(2,128)(2,1)}), bf16[1,2,2,1536,4096]{4,1,2,0,3:T(2,128)(2,1)}, u32[]{:S(2)}, u32[]{:S(2)}) %all-to-all-start.7) | async-done | bytes 50331680 | tf_op jit(solution)/shard_map/all_to_all | solution.py:68
  5654.5 43.2 copy.72
  5697.8 134.1 %gather_fusion.5 = bf16[4096,4096]{1,0:T(8,128)(2,1)} fusion(bf16[6144,4096]{1,0:T(8,128)(2,1)} %bitcast.205, s32[4096]{0:T(1024)S(1)} %copy-done.5), kind=kCustom, calls=%fused_computation.3.clone | custom fusion | bytes 67125248 | tf_op jit(solution)/shard_map/jit(_take)/gather | solution.py:69
  (114 shorter events, 822.1 us)
Async XLA Ops:
  4.5 42.2 copy-start
  4.5 42.2 copy-start.14
  46.7 41.2 copy-start.1
  212.5 41.0 copy-start.8
  284.1 29.0 copy-start.11
  341.8 28.9 copy-start.3
  632.9 45.5 copy-start.12
  632.9 52.7 copy-start.4
  685.7 85.7 %copy-start.10 = (pred[6144]{0:T(1024)(128)(4,1)S(1)}, pred[6144]{0:T(1024)(128)(4,1)}, u32[]{:S(2)}) copy-start(pred[6144]{0:T(1024)(128)(4,1)} %compare_and_fusion.1) | copy-start | bytes 18436
  804.8 12.1 copy-start.7
  804.8 41.8 copy-start.6
  804.8 555.5 %all-to-all-start = ((bf16[4,2,2,384,4096]{4,3,2,1,0:T(8,128)(2,1)}), bf16[4,2,2,384,4096]{4,3,2,1,0:T(8,128)(2,1)}, u32[]{:S(2)}, u32[]{:S(2)}) async-start(bf16[4,2,2,384,4096]{4,3,2,1,0:T(8,128)(2,1)} %bitcast.210), calls=%async_computation | async-start | bytes 100663296 | tf_op jit(solution)/shard_map/all_to_all | solution.py:64
  1360.3 554.0 %all-to-all-start.4 = ((bf16[4,2,2,384,4096]{4,3,2,1,0:T(8,128)(2,1)}), bf16[4,2,2,384,4096]{4,3,2,1,0:T(8,128)(2,1)}, u32[]{:S(2)}, u32[]{:S(2)}) async-start(bf16[4,2,2,384,4096]{4,3,2,1,0:T(8,128)(2,1)} %bitcast.211), calls=%async_computation.4 | async-start | bytes 100663296 | tf_op jit(solution)/shard_map/all_to_all | solution.py:64
  1914.3 560.7 %all-to-all-start.1 = ((bf16[1,2,2,1536,4096]{4,3,2,0,1:T(8,128)(2,1)}), bf16[1,2,2,1536,4096]{4,3,2,0,1:T(8,128)(2,1)}, u32[]{:S(2)}, u32[]{:S(2)}) async-start(bf16[1,2,2,1536,4096]{4,3,2,0,1:T(8,128)(2,1)} %bitcast.208), calls=%async_computation.1 | async-start | bytes 100663296 | tf_op jit(solution)/shard_map/all_to_all | solution.py:65
  2475.0 559.7 %all-to-all-start.5 = ((bf16[1,2,2,1536,4096]{4,3,2,0,1:T(8,128)(2,1)}), bf16[1,2,2,1536,4096]{4,3,2,0,1:T(8,128)(2,1)}, u32[]{:S(2)}, u32[]{:S(2)}) async-start(bf16[1,2,2,1536,4096]{4,3,2,0,1:T(8,128)(2,1)} %bitcast.207), calls=%async_computation.5 | async-start | bytes 100663296 | tf_op jit(solution)/shard_map/all_to_all | solution.py:65
  3429.2 559.0 %all-to-all-start.2 = ((bf16[1,1,2,3072,4096]{4,2,1,0,3:T(2,128)(2,1)}), bf16[1,1,2,3072,4096]{4,2,1,0,3:T(2,128)(2,1)}, u32[]{:S(2)}, u32[]{:S(2)}) async-start(bf16[1,1,2,3072,4096]{4,2,1,0,3:T(2,128)(2,1)} %copy.55), calls=%async_computation.2 | async-start | bytes 100663296 | tf_op jit(solution)/shard_map/all_to_all | solution.py:67
  3988.2 558.2 %all-to-all-start.6 = ((bf16[1,1,2,3072,4096]{4,2,1,0,3:T(2,128)(2,1)}), bf16[1,1,2,3072,4096]{4,2,1,0,3:T(2,128)(2,1)}, u32[]{:S(2)}, u32[]{:S(2)}) async-start(bf16[1,1,2,3072,4096]{4,2,1,0,3:T(2,128)(2,1)} %copy.70), calls=%async_computation.6 | async-start | bytes 100663296 | tf_op jit(solution)/shard_map/all_to_all | solution.py:67
  4546.4 554.0 %all-to-all-start.3 = ((bf16[1,2,2,1536,4096]{4,1,2,0,3:T(2,128)(2,1)}), bf16[1,2,2,1536,4096]{4,1,2,0,3:T(2,128)(2,1)}, u32[]{:S(2)}, u32[]{:S(2)}) async-start(bf16[1,2,2,1536,4096]{4,1,2,0,3:T(2,128)(2,1)} %bitcast.209), calls=%async_computation.3 | async-start | bytes 100663296 | tf_op jit(solution)/shard_map/all_to_all | solution.py:68
  5100.4 11.9 copy-start.9
  5100.4 554.1 %all-to-all-start.7 = ((bf16[1,2,2,1536,4096]{4,1,2,0,3:T(2,128)(2,1)}), bf16[1,2,2,1536,4096]{4,1,2,0,3:T(2,128)(2,1)}, u32[]{:S(2)}, u32[]{:S(2)}) async-start(bf16[1,2,2,1536,4096]{4,1,2,0,3:T(2,128)(2,1)} %bitcast.206), calls=%async_computation.7 | async-start | bytes 100663296 | tf_op jit(solution)/shard_map/all_to_all | solution.py:68
  5654.5 43.2 copy-start.5
  5697.8 134.1 %copy-start.2 = (f32[512,8]{1,0:T(8,128)S(1)}, f32[512,8]{1,0:T(8,128)}, u32[]{:S(2)}) copy-start(f32[512,8]{1,0:T(8,128)} %copy.64) | copy-start | bytes 49156
  5697.8 134.1 %copy-start.13 = (pred[4096]{0:T(1024)(128)(4,1)S(1)}, pred[4096]{0:T(1024)(128)(4,1)}, u32[]{:S(2)}) copy-start(pred[4096]{0:T(1024)(128)(4,1)} %compare_and_fusion.2) | copy-start | bytes 12292
where the time goes:
time: 5890 us; the launch traced here: 5870 us
  waiting for transfers between devices  3240 us (55%)
  local copies, waits for them, and re-layouts  1130 us (19%)
  matrix products  995 us (17%)
  other arithmetic  391 us (7%)
  starting transfers between devices  122 us (2%)
    all_to_all x2, waiting for transfers between devices, micro_step(): across_ep = lax.all_to_all(send_buf, 'ep', 0, 3, tiled=True)  847 us
    all_to_all x2, waiting for transfers between devices, micro_step(): arrived = lax.all_to_all(across_ep, 'sub', 1, 3, tiled=True)  840 us
    all_to_all x2, waiting for transfers between devices, micro_step(): lax.all_to_all(expert_out.reshape(1, 1, exp_local, -1, model_dim), 'sub',...  807 us
    all_to_all x2, waiting for transfers between devices, micro_step(): returned = lax.all_to_all(back_sub, 'ep', 3, 0, tiled=True)  743 us
    gather x2, local copies, waits for them, and re-layouts, micro_step(): jnp.take(returned.reshape(num_exp * cap_slots, model_dim), slot_of, axis=0)  267 us
    dot_general x2, matrix products, expert_ffn(): jnp.einsum('enf,efd->end', act_rows, w_down, preferred_element_type=jnp.f...  188 us
    reshape x2, local copies, waits for them, and re-layouts, micro_step(): expert_out.reshape(1, 1, exp_local, -1, model_dim)  179 us
    all_to_all x2, local copies, waits for them, and re-layouts, micro_step(): lax.all_to_all(expert_out.reshape(1, 1, exp_local, -1, model_dim), 'sub',...  178 us
  transfers between devices with their start and end apart: 8, of which 8 were waited for; matrix products, arithmetic and copies ran while one was open for 19% of the time, Pallas kernels for 0%

commit v1 on v0

v1 whole, which is shorter than its diff:
```python
import functools

import jax
import jax.numpy as jnp
from jax import lax
from jax.experimental import pallas as pl
from jax.experimental.pallas import tpu as pltpu
from jax.sharding import PartitionSpec as P

NORM_EPS = 1e-6
ROW_TILE = 256
FF_TILE = 256
OUT_TILE = 256
HEADS_STEP = 4
LOG2E = 1.4426950408889634
VMEM_LIMIT = 60 * 1024 * 1024


def rms_norm(values, norm_gain):
    acc_f32 = values.astype(jnp.float32)
    inv_rms = lax.rsqrt(jnp.mean(acc_f32 * acc_f32, axis=-1, keepdims=True) + NORM_EPS)
    return (acc_f32 * inv_rms * norm_gain).astype(jnp.bfloat16)


def attention_kernel(q_ref, k_ref, v_ref, o_ref):
    heads, seq_len, head_dim = q_ref.shape
    half = seq_len // 2
    scale = head_dim ** -0.5 * LOG2E
    lower = lax.broadcasted_iota(jnp.int32, (half, half), 0) >= lax.broadcasted_iota(jnp.int32, (half, half), 1)
    for head in range(heads):
        for part in range(2):
            rows = pl.ds(part * half, half)
            keys = (part + 1) * half
            scores = lax.dot_general(q_ref[head, rows, :], k_ref[head, pl.ds(0, keys), :], (((1,), (1,)), ((), ())), preferred_element_type=jnp.float32)
            diag = jnp.where(lower, scores[:, keys - half:], -jnp.inf)
            top = jnp.max(diag, axis=-1, keepdims=True)
            if part:
                top = jnp.maximum(top, jnp.max(scores[:, :half], axis=-1, keepdims=True))
            expd = jnp.exp2((diag - top) * scale)
            total = jnp.sum(expd, axis=-1, keepdims=True)
            if part:
                exps = jnp.exp2((scores[:, :half] - top) * scale)
                total = total + jnp.sum(exps, axis=-1, keepdims=True)
            inv = 1.0 / total
            ctx = jnp.dot((expd * inv).astype(jnp.bfloat16), v_ref[head, rows, :], preferred_element_type=jnp.float32)
            if part:
                ctx = ctx + jnp.dot((exps * inv).astype(jnp.bfloat16), v_ref[head, pl.ds(0, half), :], preferred_element_type=jnp.float32)
            o_ref[rows, pl.ds(head * head_dim, head_dim)] = ctx.astype(jnp.bfloat16)


def attention_core(q_heads, k_heads, v_heads):
    heads, seq_len, head_dim = q_heads.shape
    spec = pl.BlockSpec((HEADS_STEP, seq_len, head_dim), lambda i: (i, 0, 0))
    return pl.pallas_call(
        attention_kernel,
        grid=(heads // HEADS_STEP,),
        in_specs=[spec] * 3,
        out_specs=pl.BlockSpec((seq_len, HEADS_STEP * head_dim), lambda i: (0, i)),
        out_shape=jax.ShapeDtypeStruct((seq_len, heads * head_dim), jnp.bfloat16),
        compiler_params=pltpu.CompilerParams(dimension_semantics=("arbitrary",)),
        cost_estimate=pl.CostEstimate(flops=25_000_000_000, bytes_accessed=4 * heads * seq_len * head_dim * 2, transcendentals=heads * seq_len * seq_len),
        name="attention_core",
    )(q_heads, k_heads, v_heads)


def attention_block(tokens, attn_norm, w_query, w_key, w_value, w_out, moe_norm):
    seq_len, model_dim = tokens.shape
    normed = rms_norm(tokens, attn_norm)
    q_heads = jnp.einsum('sd,dhc->hsc', normed, w_query, preferred_element_type=jnp.float32).astype(jnp.bfloat16)
    k_heads = jnp.einsum('sd,dhc->hsc', normed, w_key, preferred_element_type=jnp.float32).astype(jnp.bfloat16)
    v_heads = jnp.einsum('sd,dhc->hsc', normed, w_value, preferred_element_type=jnp.float32).astype(jnp.bfloat16)
    context = attention_core(q_heads, k_heads, v_heads)
    proj_out = jnp.dot(context, w_out.reshape(-1, model_dim), preferred_element_type=jnp.float32)
    hidden = (tokens.astype(jnp.float32) + proj_out).astype(jnp.bfloat16)
    return hidden, rms_norm(hidden, moe_norm)


def expert_in_kernel(sources, offs_ref, rank_ref, z_ref, gate_ref, up_ref, u_ref, rows_ref):
    step = pl.program_id(0)
    room = rank_ref.shape[2] * 3 // 4
    toks = rank_ref.shape[2]
    model_dim = z_ref.shape[1]

    @pl.when(step < sources)
    def _():
        base = pl.multiple_of(offs_ref[step], 16)
        pick = (lax.broadcasted_iota(jnp.int32, (room, toks), 0) == rank_ref[0]).astype(jnp.float32).astype(jnp.bfloat16)
        for part in range(4):
            cols = pl.ds(part * (model_dim // 4), model_dim // 4)
            rows_ref[pl.ds(base, room), cols] = jnp.dot(pick, z_ref[:, cols], preferred_element_type=jnp.float32).astype(jnp.bfloat16)

    @pl.when(step == sources - 1)
    def _():
        end = pl.multiple_of(offs_ref[sources], 16)
        rows_ref[pl.ds(end, ROW_TILE), :] = jnp.zeros((ROW_TILE, model_dim), jnp.bfloat16)

    @pl.when(step >= sources)
    def _():
        def tile(index, carry):
            rows = pl.ds(pl.multiple_of(index * ROW_TILE, ROW_TILE), ROW_TILE)
            block = rows_ref[rows, :]
            gate_h = jnp.dot(block, gate_ref[0], preferred_element_type=jnp.float32)
            up_h = jnp.dot(block, up_ref[0], preferred_element_type=jnp.float32)
            u_ref[0, rows, :] = (gate_h * jax.nn.sigmoid(gate_h) * up_h).astype(jnp.bfloat16)
            return carry

        lax.fori_loop(0, (offs_ref[sources] + ROW_TILE - 1) // ROW_TILE, tile, 0)


def expert_in(offs, rank_rows, z_all, w_gate, w_up):
    experts, model_dim, ff_dim = w_gate.shape
    sources, _, toks = rank_rows.shape
    room = sources * toks * 3 // 4
    ff_tiles = ff_dim // FF_TILE

    def weight_map(i, offs_ref):
        j = jnp.maximum(i - sources, 0)
        return (j // ff_tiles, 0, j % ff_tiles)

    return pl.pallas_call(
        functools.partial(expert_in_kernel, sources),
        grid_spec=pltpu.PrefetchScalarGridSpec(
            num_scalar_prefetch=1,
            grid=(sources + experts * ff_tiles,),
            in_specs=[
                pl.BlockSpec((1, 1, toks), lambda i, offs_ref: (jnp.minimum(i, sources - 1), 0, 0)),
                pl.BlockSpec((toks, model_dim), lambda i, offs_ref: (jnp.minimum(i, sources - 1), 0)),
                pl.BlockSpec((1, model_dim, FF_TILE), weight_map),
                pl.BlockSpec((1, model_dim, FF_TILE), weight_map),
            ],
            out_specs=pl.BlockSpec((1, room, FF_TILE), weight_map),
            scratch_shapes=[pltpu.VMEM((room + ROW_TILE, model_dim), jnp.bfloat16)],
        ),
        out_shape=jax.ShapeDtypeStruct((experts, room, ff_dim), jnp.bfloat16),
        compiler_params=pltpu.CompilerParams(dimension_semantics=("arbitrary",), vmem_limit_bytes=VMEM_LIMIT),
        cost_estimate=pl.CostEstimate(flops=130_000_000_000, bytes_accessed=120_000_000, transcendentals=room * ff_dim * experts),
        name="expert_in",
    )(offs, rank_rows, z_all, w_gate, w_up)


def expert_out_kernel(sources, offs_ref, cols_ref, u_ref, down_ref, out_ref, e_ref, place_ref):
    step = pl.program_id(0)
    experts = u_ref.shape[0]
    toks = out_ref.shape[0] // sources
    room = place_ref.shape[2]

    @pl.when(step == 0)
    def _():
        e_ref[...] = jnp.zeros_like(e_ref)
        for source in range(sources):
            rank = cols_ref[pl.ds(source * toks, toks), experts:experts + 1]
            spots = lax.broadcasted_iota(jnp.int32, (toks, room), 1).astype(jnp.float32)
            place_ref[source] = (spots == rank).astype(jnp.float32).astype(jnp.bfloat16)

    def tile(index, carry):
        rows = pl.ds(pl.multiple_of(index * ROW_TILE, ROW_TILE), ROW_TILE)
        for expert in range(experts):
            e_ref[expert, rows, :] = jnp.dot(u_ref[expert, rows, :], down_ref[expert], preferred_element_type=jnp.float32).astype(jnp.bfloat16)
        return carry

    lax.fori_loop(0, (offs_ref[sources] + ROW_TILE - 1) // ROW_TILE, tile, 0)

    def spread(source, carry):
        base = pl.multiple_of(offs_ref[source], 16)
        toks_at = pl.ds(pl.multiple_of(source * toks, toks), toks)
        total = jnp.zeros((toks, out_ref.shape[1]), jnp.float32)
        for expert in range(experts):
            values = jnp.dot(place_ref[source], e_ref[expert, pl.ds(base, room), :], preferred_element_type=jnp.float32)
            total = total + cols_ref[toks_at, expert:expert + 1] * values
        out_ref[toks_at, :] = total
        return carry

    lax.fori_loop(0, sources, spread, 0)


def expert_out(offs, cols, u_rows, w_down):
    experts, ff_dim, model_dim = w_down.shape
    sources = offs.shape[0] - 1
    tok_total = cols.shape[0]
    toks = tok_total // sources
    room = toks * 3 // 4
    return pl.pallas_call(
        functools.partial(expert_out_kernel, sources),
        grid_spec=pltpu.PrefetchScalarGridSpec(
            num_scalar_prefetch=1,
            grid=(model_dim // OUT_TILE,),
            in_specs=[
                pl.BlockSpec((tok_total, cols.shape[1]), lambda i, offs_ref: (0, 0), pipeline_mode=pl.Buffered(1)),
                pl.BlockSpec(u_rows.shape, lambda i, offs_ref: (0, 0, 0), pipeline_mode=pl.Buffered(1)),
                pl.BlockSpec((experts, ff_dim, OUT_TILE), lambda i, offs_ref: (0, 0, i)),
            ],
            out_specs=pl.BlockSpec((tok_total, OUT_TILE), lambda i, offs_ref: (0, i)),
            scratch_shapes=[
                pltpu.VMEM((experts, u_rows.shape[1], OUT_TILE), jnp.bfloat16),
                pltpu.VMEM((sources, toks, room), jnp.bfloat16),
            ],
        ),
        out_shape=jax.ShapeDtypeStruct((tok_total, model_dim), jnp.float32),
        compiler_params=pltpu.CompilerParams(dimension_semantics=("arbitrary",), vmem_limit_bytes=VMEM_LIMIT),
        cost_estimate=pl.CostEstimate(flops=90_000_000_000, bytes_accessed=120_000_000, transcendentals=0),
        name="expert_out",
    )(offs, cols, u_rows, w_down)


def route_tables(route_idx, route_gate, axes, groups, exp_local):
    micro, toks, _ = route_idx.shape
    num_exp = groups * exp_local
    hit = route_idx[:, :, :, None] == jnp.arange(num_exp, dtype=jnp.int32)
    gates = jnp.sum(jnp.where(hit, route_gate[:, :, :, None], 0.0), axis=2)
    seen = jnp.any(hit, axis=2).astype(jnp.float32)
    gates = gates.transpose(2, 0, 1).reshape(groups, exp_local, micro * toks)
    seen = seen.transpose(2, 0, 1).reshape(groups, exp_local, micro * toks)[:, :1]
    table = jnp.concatenate([gates, seen], axis=1).reshape(groups * (exp_local + 1), micro * toks)
    table = lax.all_to_all(table, axes, 0, 0, tiled=True)
    table = table.reshape(groups, exp_local + 1, micro, toks).transpose(2, 0, 1, 3)
    seen = table[:, :, exp_local]
    before = (jnp.arange(toks)[:, None] < jnp.arange(toks)[None, :]).astype(jnp.bfloat16)
    rank = jnp.einsum('mgt,ts->mgs', seen.astype(jnp.bfloat16), before, preferred_element_type=jnp.float32)
    rank = jnp.where(seen > 0, rank, -1.0)
    held = (jnp.sum(seen, axis=-1).astype(jnp.int32) + 15) // 16 * 16
    upto = (jnp.arange(groups + 1)[:, None] > jnp.arange(groups)[None, :]).astype(jnp.int32)
    offs = jnp.sum(held[:, None, :] * upto[None], axis=-1)
    cols = jnp.concatenate([table[:, :, :exp_local], rank[:, :, None]], axis=2).transpose(0, 1, 3, 2).reshape(micro, groups * toks, exp_local + 1)
    return offs, rank.astype(jnp.int32)[:, :, None, :], cols


def solution(mesh):
    axes = ('ep', 'sub')
    groups = mesh.shape['ep'] * mesh.shape['sub']
    tok_spec = P(('dp', 'ep', 'sub'), None, None)
    route_spec = P(None, ('dp', 'ep', 'sub'), None)
    exp_spec = P(('ep', 'sub'), None, None)

    def device_body(input_a, input_b, route_idx, route_gate, attn_norm, w_query, w_key, w_value, w_out, moe_norm, w_gate, w_up, w_down):
        offs, rank_rows, cols = route_tables(route_idx, route_gate, axes, groups, w_gate.shape[0])
        hidden, gathered = [], []
        for tokens in (input_a, input_b):
            h, z = attention_block(tokens[0], attn_norm, w_query, w_key, w_value, w_out, moe_norm)
            hidden.append(h)
            gathered.append(lax.all_gather(z, axes, axis=0, tiled=True))
        outs = []
        for m in range(2):
            u_rows = expert_in(offs[m], rank_rows[m], gathered[m], w_gate, w_up)
            partial = expert_out(offs[m], cols[m], u_rows, w_down)
            moe_sum = lax.psum_scatter(partial, axes, scatter_dimension=0, tiled=True)
            outs.append((hidden[m].astype(jnp.float32) + moe_sum).astype(jnp.bfloat16)[None])
        return tuple(outs)

    return jax.shard_map(device_body, mesh=mesh, in_specs=(tok_spec, tok_spec, route_spec, route_spec, P(), P(), P(), P(), P(), P(), exp_spec, exp_spec, exp_spec), out_specs=(tok_spec, tok_spec), check_vma=False)
```

time: 5890 us -> 1710 us (0.29)
  waiting for transfers between devices: 3240 us -> 607 us
  local copies, waits for them, and re-layouts: 1130 us -> 7.03 us
  Pallas kernels: 0 us -> 707 us
  matrix products: 995 us -> 339 us
  other arithmetic: 391 us -> 28.4 us
  starting transfers between devices: 122 us -> 4.44 us
    all_to_all x8 -> x1, waiting for transfers between devices: 3240 us -> 4.91 us  [route_tables(): table = lax.all_to_all(table, axes, 0, 0, tiled=True)]
    pallas_call x0 -> x6, Pallas kernels: none -> 707 us  [the longest x2 304 us: expert_in(): pl.pallas_call(functools.partial(expert_in_kernel, sources), grid_spec=pl...]
    dot_general x18 -> x9, matrix products: 995 us -> 339 us  [the longest x2 90.6 us: attention_block(): jnp.dot(context, w_out.reshape(-1, model_dim), preferred_element_type=jnp...]
    gather x8 -> x0, local copies, waits for them, and re-layouts: 486 us -> none  [the longest x2 267 us: micro_step(): jnp.take(returned.reshape(num_exp * cap_slots, model_dim), slot_of, axis=0)]
    reduce_scatter x0 -> x2, waiting for transfers between devices: none -> 459 us  [device_body(): moe_sum = lax.psum_scatter(partial, axes, scatter_dimension=0, tiled=True)]
    all_to_all x8 -> x0, local copies, waits for them, and re-layouts: 398 us -> none  [the longest x2 178 us: micro_step(): lax.all_to_all(expert_out.reshape(1, 1, exp_local, -1, model_dim), 'sub',...]
    reshape x2 -> x4, local copies, waits for them, and re-layouts: 179 us -> 0.24 us  [the longest x2 0.11 us: route_tables(): table.reshape(groups, exp_local + 1, micro, toks).transpose(2, 0, 1, 3)]
    all_gather x0 -> x2, waiting for transfers between devices: none -> 142 us  [device_body(): gathered.append(lax.all_gather(z, axes, axis=0, tiled=True))]
  transfers between devices with their start and end apart: 8 -> 5, of which waited for: 8 -> 4; matrix products, arithmetic and copies ran while one was open for 19% -> 1% of each run, Pallas kernels for 0% -> 35%
where the time goes in v1:
time: 1710 us
  Pallas kernels  707 us (41%)
  waiting for transfers between devices  607 us (35%)
  matrix products  339 us (20%)
  other arithmetic  28.4 us (2%)
    reduce_scatter x2, waiting for transfers between devices, device_body(): moe_sum = lax.psum_scatter(partial, axes, scatter_dimension=0, tiled=True)  459 us
    pallas_call x2, Pallas kernels, expert_in(): pl.pallas_call(functools.partial(expert_in_kernel, sources), grid_spec=pl...  304 us
    pallas_call x2, Pallas kernels, expert_out(): pl.pallas_call(functools.partial(expert_out_kernel, sources), grid_spec=p...  293 us
    all_gather x2, waiting for transfers between devices, device_body(): gathered.append(lax.all_gather(z, axes, axis=0, tiled=True))  142 us
    pallas_call x2, Pallas kernels, attention_core(): pl.pallas_call(attention_kernel, grid=(heads // HEADS_STEP,), in_specs=[s...  111 us
    dot_general x2, matrix products, attention_block(): jnp.dot(context, w_out.reshape(-1, model_dim), preferred_element_type=jnp...  90.6 us
    dot_general x2, matrix products, attention_block(): jnp.einsum('sd,dhc->hsc', normed, w_value, preferred_element_type=jnp.flo...  83.4 us
    dot_general x2, matrix products, attention_block(): jnp.einsum('sd,dhc->hsc', normed, w_query, preferred_element_type=jnp.flo...  82.3 us
  transfers between devices with their start and end apart: 5, of which 4 were waited for; matrix products, arithmetic and copies ran while one was open for 1% of the time, Pallas kernels for 35%

profile of v1, /device:TPU:0, one launch (start us, length us, event | category | flops | bytes accessed | tf_op | source)
XLA Modules:
  0.0 1707.3 jit_solution(890755509164885828)
XLA Ops:
  7.2 3.1 fusion.24
  10.3 42.2 %convert_bitcast_fusion.v_ref = bf16[64,512,128]{2,1,0:T(8,128)(2,1)} fusion(bf16[4096,64,128]{2,1,0:T(8,128)(2,1)} %param.20, bf16[1,512,4096]{2,1,0:T(8,128)(2,1)} %param.14, f32[512]{0:T(512)S(1)} %add_rsqrt_fusion.1, f32[4096]{0:T(1024)} %param.17), kind=kOutput, calls=%fused_computation.40 | convolution fusion | flops 34372321280 | bytes 79710208 | tf_op jit(solution)/shard_map/sd,dhc->hsc/dot_general | solution.py:71
  52.6 41.1 %convert_bitcast_fusion.1.k_ref = bf16[64,512,128]{2,1,0:T(8,128)(2,1)} fusion(bf16[4096,64,128]{2,1,0:T(8,128)(2,1)} %param.19, bf16[1,512,4096]{2,1,0:T(8,128)(2,1)S(1)} %copy-done, f32[512]{0:T(512)S(1)} %add_rsqrt_fusion.1, f32[4096]{0:T(1024)S(1)} %copy-done.6), kind=kOutput, calls=%fused_computation.41 | convolution fusion | flops 34372321280 | bytes 79710208 | tf_op jit(solution)/shard_map/sd,dhc->hsc/dot_general | solution.py:70
  93.7 0.9 fusion.20
  94.6 41.2 %convert_bitcast_fusion.3.v_ref = bf16[64,512,128]{2,1,0:T(8,128)(2,1)} fusion(bf16[4096,64,128]{2,1,0:T(8,128)(2,1)} %param.20, bf16[1,512,4096]{2,1,0:T(8,128)(2,1)S(1)} %copy-done.1, f32[4096]{0:T(1024)S(1)} %copy-done.6, f32[512]{0:T(512)S(1)} %add_rsqrt_fusion.3), kind=kOutput, calls=%fused_computation.43 | convolution fusion | flops 34372321280 | bytes 79710208 | tf_op jit(solution)/shard_map/sd,dhc->hsc/dot_general | solution.py:71
  135.8 41.0 %convert_bitcast_fusion.4.k_ref = bf16[64,512,128]{2,1,0:T(8,128)(2,1)} fusion(bf16[4096,64,128]{2,1,0:T(8,128)(2,1)} %param.19, bf16[1,512,4096]{2,1,0:T(8,128)(2,1)S(1)} %copy-done.1, f32[4096]{0:T(1024)S(1)} %copy-done.6, f32[512]{0:T(512)S(1)} %add_rsqrt_fusion.3), kind=kOutput, calls=%fused_computation.44 | convolution fusion | flops 34372321280 | bytes 79710208 | tf_op jit(solution)/shard_map/sd,dhc->hsc/dot_general | solution.py:70
  176.8 41.4 %convert_bitcast_fusion.2.q_ref = bf16[64,512,128]{2,1,0:T(8,128)(2,1)} fusion(bf16[4096,64,128]{2,1,0:T(8,128)(2,1)} %param.18, bf16[1,512,4096]{2,1,0:T(8,128)(2,1)S(1)} %copy-done, f32[512]{0:T(512)S(1)} %add_rsqrt_fusion.1, f32[4096]{0:T(1024)S(1)} %copy-done.6), kind=kOutput, calls=%fused_computation.42 | convolution fusion | flops 34372321280 | bytes 79710208 | tf_op jit(solution)/shard_map/sd,dhc->hsc/dot_general | solution.py:69
  218.2 41.0 %convert_bitcast_fusion.5.q_ref = bf16[64,512,128]{2,1,0:T(8,128)(2,1)} fusion(bf16[4096,64,128]{2,1,0:T(8,128)(2,1)} %param.18, bf16[1,512,4096]{2,1,0:T(8,128)(2,1)S(1)} %copy-done.1, f32[4096]{0:T(1024)S(1)} %copy-done.6, f32[512]{0:T(512)S(1)} %add_rsqrt_fusion.3), kind=kOutput, calls=%fused_computation.45 | convolution fusion | flops 34372321280 | bytes 79710208 | tf_op jit(solution)/shard_map/sd,dhc->hsc/dot_general | solution.py:69
  259.1 55.4 %attention_core.3 = bf16[512,8192]{1,0:T(8,128)(2,1)} custom-call(bf16[64,512,128]{2,1,0:T(8,128)(2,1)} %convert_bitcast_fusion.2.q_ref, bf16[64,512,128]{2,1,0:T(8,128)(2,1)} %convert_bitcast_fusion.1.k_ref, bf16[64,512,128]{2,1,0:T(8,128)(2,1)} %convert_bitcast_fusion.v_ref), custom_call_target="tpu_custom_call" | custom-call | flops 24999999488 | bytes 33554432 | tf_op jit(solution)/shard_map/attention_core/pallas_call | solution.py:54
  314.6 45.3 %fusion.16 = (f32[512]{0:T(512)S(1)}, bf16[512,4096]{1,0:T(8,128)(2,1)}) fusion(bf16[512,8192]{1,0:T(8,128)(2,1)} %attention_core.3, bf16[8192,4096]{1,0:T(8,128)(2,1)} %bitcast.6, bf16[1,512,4096]{2,1,0:T(8,128)(2,1)} %param.14), kind=kOutput, calls=%fused_computation.28 | convolution fusion | flops 34372321280 | bytes 83888128 | tf_op jit(solution)/shard_map/dot_general | solution.py:73
  359.8 55.4 %attention_core.2 = bf16[512,8192]{1,0:T(8,128)(2,1)} custom-call(bf16[64,512,128]{2,1,0:T(8,128)(2,1)} %convert_bitcast_fusion.5.q_ref, bf16[64,512,128]{2,1,0:T(8,128)(2,1)} %convert_bitcast_fusion.4.k_ref, bf16[64,512,128]{2,1,0:T(8,128)(2,1)} %convert_bitcast_fusion.3.v_ref), custom_call_target="tpu_custom_call" | custom-call | flops 24999999488 | bytes 33554432 | tf_op jit(solution)/shard_map/attention_core/pallas_call | solution.py:54
  415.3 45.3 %fusion.12 = (f32[512]{0:T(512)S(1)}, bf16[512,4096]{1,0:T(8,128)(2,1)}) fusion(bf16[512,8192]{1,0:T(8,128)(2,1)} %attention_core.2, bf16[8192,4096]{1,0:T(8,128)(2,1)} %bitcast.6, bf16[1,512,4096]{2,1,0:T(8,128)(2,1)} %param.13), kind=kOutput, calls=%fused_computation.24 | convolution fusion | flops 34372321280 | bytes 83888128 | tf_op jit(solution)/shard_map/dot_general | solution.py:73
  460.6 7.2 fusion.18
  467.9 0.7 all-gather.3.cloned.1.call-update
  469.1 0.7 pad_maximum_fusion
  469.8 4.3 all-to-all-start
  474.1 4.9 all-to-all-done
  479.7 0.7 fusion.62
  480.4 2.0 copy.55
  482.5 0.5 slice_bitcast_fusion.2
  483.0 0.6 slice_bitcast_fusion
  483.7 142.3 %all-gather.5.cloned.1.call-done.z_ref = bf16[4096,4096]{1,0:T(8,128)(2,1)} async-done(((bf16[512,4096]{1,0:T(8,128)(2,1)}), bf16[4096,4096]{1,0:T(8,128)(2,1)}) %all-gather.5.cloned.1.call-update) | async-done | bytes 33554448 | tf_op jit(solution)/shard_map/all_gather | solution.py:240
  626.0 145.4 %expert_in.3.u_ref = bf16[2,3072,1536]{2,1,0:T(8,128)(2,1)} custom-call(s32[9]{0:T(128)} %get-tuple-element.10.offs_ref, s32[8,1,512]{2,1,0:T(1,128)} %get-tuple-element.6.rank_ref, bf16[4096,4096]{1,0:T(8,128)(2,1)} %all-gather.5.cloned.1.call-done.z_ref, bf16[2,4096,1536]{2,1,0:T(8,128)(2,1)} %gate_ref.3, bf16[2,4096,1536]{2,1,0:T(8,128)(2,1)} %up_ref.3), custom_call_target="tpu_custom_call" | custom-call | flops 130000003072 | bytes 120000000 | tf_op jit(solution)/shard_map/expert_in/pallas_call | solution.py:120
  771.3 141.5 %expert_out.3 = f32[4096,4096]{1,0:T(8,128)} custom-call(s32[9]{0:T(128)} %get-tuple-element.10.offs_ref, f32[4096,3]{1,0:T(8,128)} %bitcast.77, bf16[2,3072,1536]{2,1,0:T(8,128)(2,1)} %expert_in.3.u_ref, bf16[2,1536,4096]{2,1,0:T(8,128)(2,1)} %down_ref.3), custom_call_target="tpu_custom_call" | custom-call | flops 89999998976 | bytes 120000000 | tf_op jit(solution)/shard_map/expert_out/pallas_call | solution.py:182
  912.9 0.7 copy-done.2
  913.6 1.9 copy.57
  915.5 158.3 %expert_in.2.u_ref = bf16[2,3072,1536]{2,1,0:T(8,128)(2,1)} custom-call(s32[9]{0:T(128)} %get-tuple-element.11.offs_ref, s32[8,1,512]{2,1,0:T(1,128)} %get-tuple-element.7.rank_ref, bf16[4096,4096]{1,0:T(8,128)(2,1)} %all-gather.3.cloned.1.call-done.z_ref, bf16[2,4096,1536]{2,1,0:T(8,128)(2,1)} %gate_ref.3, bf16[2,4096,1536]{2,1,0:T(8,128)(2,1)} %up_ref.3), custom_call_target="tpu_custom_call" | custom-call | flops 130000003072 | bytes 120000000 | tf_op jit(solution)/shard_map/expert_in/pallas_call | solution.py:120
  1073.9 151.2 %expert_out.2 = f32[4096,4096]{1,0:T(8,128)} custom-call(s32[9]{0:T(128)} %get-tuple-element.11.offs_ref, f32[4096,3]{1,0:T(8,128)} %bitcast.78, bf16[2,3072,1536]{2,1,0:T(8,128)(2,1)} %expert_in.2.u_ref, bf16[2,1536,4096]{2,1,0:T(8,128)(2,1)} %down_ref.3), custom_call_target="tpu_custom_call" | custom-call | flops 89999998976 | bytes 120000000 | tf_op jit(solution)/shard_map/expert_out/pallas_call | solution.py:182
  1225.1 88.3 %reduce-scatter.5.cloned.1.call-done = f32[512,4096]{1,0:T(8,128)} async-done(((f32[4096,4096]{1,0:T(8,128)}), f32[512,4096]{1,0:T(8,128)}) %reduce-scatter.5.cloned.1.call-update) | async-done | bytes 8388624 | tf_op jit(solution)/shard_map/reduce_scatter | solution.py:245
  1313.3 8.0 fusion.42
  1321.4 371.0 %reduce-scatter.3.cloned.1.call-done = f32[512,4096]{1,0:T(8,128)} async-done(((f32[4096,4096]{1,0:T(8,128)}), f32[512,4096]{1,0:T(8,128)}) %reduce-scatter.3.cloned.1.call-update) | async-done | bytes 8388624 | tf_op jit(solution)/shard_map/reduce_scatter | solution.py:245
  1692.3 8.0 fusion.43
  (43 shorter events, 1.3 us)
Async XLA Ops:
  7.2 618.8 %all-gather.5.cloned.1.call-start = ((), (), s32[]{:S(2)}) async-start(), calls=%async_computation.5 | async-start | bytes 37748736 | tf_op jit(solution)/shard_map/all_gather | solution.py:240
  10.3 42.3 %copy-start = (bf16[1,512,4096]{2,1,0:T(8,128)(2,1)S(1)}, bf16[1,512,4096]{2,1,0:T(8,128)(2,1)}, u32[]{:S(2)}) copy-start(bf16[1,512,4096]{2,1,0:T(8,128)(2,1)} %param.14) | copy-start | bytes 12582916
  10.3 42.2 %copy-start.6 = (f32[4096]{0:T(1024)S(1)}, f32[4096]{0:T(1024)}, u32[]{:S(2)}) copy-start(f32[4096]{0:T(1024)} %param.17) | copy-start | bytes 49156
  52.6 41.2 %copy-start.1 = (bf16[1,512,4096]{2,1,0:T(8,128)(2,1)S(1)}, bf16[1,512,4096]{2,1,0:T(8,128)(2,1)}, u32[]{:S(2)}) copy-start(bf16[1,512,4096]{2,1,0:T(8,128)(2,1)} %param.13) | copy-start | bytes 12582916
  415.3 45.4 %copy-start.5 = (f32[4096]{0:T(1024)S(1)}, f32[4096]{0:T(1024)}, u32[]{:S(2)}) copy-start(f32[4096]{0:T(1024)} %param.22) | copy-start | bytes 49156
  467.9 0.8 copy-start.3
  467.9 0.8 copy-start.4
  467.9 447.7 %all-gather.3.cloned.1.call-start = ((), (), s32[]{:S(2)}) async-start(), calls=%async_computation.3 | async-start | bytes 37748736 | tf_op jit(solution)/shard_map/all_gather | solution.py:240
  469.8 9.2 all-to-all-start
  474.1 839.3 %reduce-scatter.5.cloned.1.call-start = ((), (), s32[]{:S(2)}) async-start(), calls=%async_computation.6 | async-start | bytes 75497472 | tf_op jit(solution)/shard_map/reduce_scatter | solution.py:245
  912.8 0.8 copy-start.2
  912.8 779.5 %reduce-scatter.3.cloned.1.call-start = ((), (), s32[]{:S(2)}) async-start(), calls=%async_computation.4 | async-start | bytes 75497472 | tf_op jit(solution)/shard_map/reduce_scatter | solution.py:245
Sparse Core Ops, SparseCore 0:
  468.0 157.8 all-gather.4
  627.8 155.0 all-gather.2
  912.9 400.3 reduce-scatter.4
  1316.7 375.6 reduce-scatter.2
